TPU v7x, 32 devices: a whole 2x2x4 slice. The times are simulated.
32 devices in a mesh: grp: 1, exp: 32 (over z, y, x, core).
Axes of the slice: x: 2, y: 2, z: 4, core: 2. Of those that a mesh axis runs over, the one named last changes fastest.
Arguments:
- tokens: bfloat16 [512, 2048], P(('grp', 'exp')), may hold values from -6 to 6
- routed_expert_index: int32 [512, 6], P(('grp', 'exp')), may hold values from 0 to 15, all different within a row; in each aligned block of 16 rows (0 to 15, 16 to 31, ...) at most 8 rows name the same one
- routing_gate_weight: float32 [512, 6], P(('grp', 'exp')), may hold values from 0.05 to 0.5
- token_adapter_index: int32 [512], P('grp'), may hold values from 0 to 511
- gate_weight_pieces: bfloat16 [32, 2048, 704], P('exp'), may hold values from -0.125 to 0.125
- up_weight: bfloat16 [32, 2048, 704], P('exp'), may hold values from -0.125 to 0.125
- down_weight: bfloat16 [32, 704, 2048], P('exp'), may hold values from -0.15625 to 0.15625
- adapter_down_matrix: bfloat16 [2048, 8192], P('exp'), may hold values from -0.125 to 0.125
- adapter_up_matrix: bfloat16 [2048, 8192], P('exp'), may hold values from -1.5 to 1.5
Outputs:
- mixed: bfloat16 [512, 2048], P(('grp', 'exp'))
Inputs may be any that keep to these rules, and one draw needn't show every extreme that they name: `routed_expert_index`: each token names 6 different experts; among the 16 tokens of one index of exp (aligned blocks of rows) no expert is named more than 8 times.
All inputs are finite; a program needn't handle non-finite values.
Results may differ from a plain program's by a relative error of at most 0.009.
Values may be sent and summed in bfloat16 or wider, within the bound.
A program may use at most 128 MiB of HBM per device.

v0:
```python
import jax
import jax.numpy as jnp
from jax import lax
from jax.sharding import PartitionSpec as P

TOP = 6
ADAPTER_RANK = 16


def expert_half(row_block, gate_weight_pieces, up_weight, down_weight):
    gate_act = jnp.dot(row_block, gate_weight_pieces[0], preferred_element_type=jnp.float32)
    up_act = jnp.dot(row_block, up_weight[0], preferred_element_type=jnp.float32)
    hidden = (jax.nn.silu(gate_act) * up_act).astype(jnp.bfloat16)
    return jnp.dot(hidden, down_weight[0], preferred_element_type=jnp.float32)


def per_device(
    tokens,
    routed_expert_index,
    routing_gate_weight,
    token_adapter_index,
    gate_weight_pieces,
    up_weight,
    down_weight,
    adapter_down_matrix,
    adapter_up_matrix,
):
    devices = lax.axis_size("exp")
    experts = devices // 2
    tok_dev = tokens.shape[0]
    model_width = tokens.shape[1]
    capacity = 2 * (tok_dev * TOP // devices + 1)
    flat_ids = routed_expert_index.reshape(-1)
    gate_col = routing_gate_weight.reshape(-1, 1)
    one_hot = (flat_ids[:, None] == jnp.arange(experts, dtype=jnp.int32)[None, :]).astype(jnp.int32)
    counted = jnp.cumsum(one_hot, axis=0)
    position = jnp.sum(one_hot * counted, axis=1) - 1
    slots = flat_ids * capacity + position
    token_rows = jnp.repeat(tokens, TOP, axis=0)
    buffer = jnp.zeros((experts * capacity, model_width), tokens.dtype).at[slots].set(token_rows)
    buffer, slots = (buffer, slots)
    doubled = jnp.broadcast_to(
        buffer.reshape(experts, 1, capacity, model_width), (experts, 2, capacity, model_width)
    )
    doubled = doubled.reshape(devices, capacity, model_width)
    received = lax.all_to_all(doubled, "exp", split_axis=0, concat_axis=0, tiled=True)
    sources = received.shape[0]
    items = received.shape[1]
    output = expert_half(
        received.reshape(sources * items, model_width), gate_weight_pieces, up_weight, down_weight
    )
    partial_value = output.reshape(sources, items, model_width)
    returned = lax.all_to_all(
        partial_value.astype(jnp.bfloat16), "exp", split_axis=0, concat_axis=0, tiled=True
    ).astype(partial_value.dtype)
    results = jnp.sum(returned.reshape(experts, 2, capacity, model_width), axis=1)
    gather_results = results.reshape(experts * capacity, model_width)
    picked = gather_results[slots] * gate_col
    routed = jnp.sum(picked.reshape(tok_dev, TOP, model_width), axis=1)
    columns = lax.all_to_all(tokens, "exp", split_axis=1, concat_axis=0, tiled=True)
    feature_rows = adapter_down_matrix.shape[0]
    adapter_table = adapter_down_matrix.shape[1] // ADAPTER_RANK
    down_selected = adapter_down_matrix.reshape(feature_rows, adapter_table, ADAPTER_RANK)[
        :, token_adapter_index, :
    ]
    rank_terms = jnp.einsum(
        "tf,ftr->tr", columns, down_selected, preferred_element_type=jnp.float32
    )
    gathered_ranks = lax.psum(rank_terms, "exp").astype(jnp.bfloat16)
    up_selected = adapter_up_matrix.reshape(feature_rows, adapter_table, ADAPTER_RANK)[
        :, token_adapter_index, :
    ]
    correction_cols = jnp.einsum(
        "tr,ftr->tf", gathered_ranks, up_selected, preferred_element_type=jnp.float32
    )
    lowrank_delta = lax.all_to_all(
        correction_cols.astype(jnp.bfloat16), "exp", split_axis=0, concat_axis=1, tiled=True
    )
    return (routed + lowrank_delta.astype(jnp.float32)).astype(jnp.bfloat16)


def solution(mesh):
    placed = (
        P(("grp", "exp"), None),
        P(("grp", "exp"), None),
        P(("grp", "exp"), None),
        P("grp"),
        P("exp", None, None),
        P("exp", None, None),
        P("exp", None, None),
        P("exp", None),
        P("exp", None),
    )
    return jax.shard_map(
        per_device, mesh=mesh, in_specs=placed, out_specs=P(("grp", "exp"), None), check_vma=False
    )
```

profile of v0, /device:TPU:0, one launch (start us, length us, event | category | flops | bytes accessed | tf_op | source)
XLA Modules:
  0.0 140.4 jit_solution(14712672242584712208)
XLA Ops:
  0.0 0.0 copy-start
  0.0 1.2 all_to_all.32
  1.2 0.1 copy.38
  1.2 0.8 reshape.132
  2.0 7.3 %all-to-all-start.2 = ((bf16[32,2,512]{2,1,0:T(2,128)(2,1)}), bf16[32,2,512]{2,1,0:T(2,128)(2,1)S(1)}, u32[]{:S(2)}, u32[]{:S(2)}) async-start(bf16[32,2,512]{2,1,0:T(2,128)(2,1)} %reshape.132), calls=%async_computation.2 | async-start | bytes 131072 | tf_op jit(solution)/shard_map/all_to_all | solution.py:60
  9.3 0.7 broadcast_multiply_fusion
  10.0 0.8 copy.22
  10.8 0.1 copy.21
  10.9 0.1 mul.37
  11.0 0.1 eq.15
  11.1 0.1 fusion.26
  11.2 0.1 reduce_window_sum.11
  11.3 0.2 select_reduce_fusion
  11.5 0.9 broadcast_in_dim.21
  12.4 0.9 reshape.119
  13.3 1.8 %scatter_custom_fusion = bf16[128,2048]{1,0:T(8,128)(2,1)S(1)} fusion(s32[96]{0:T(128)S(1)} %fusion.27, bf16[96,2048]{1,0:T(8,128)(2,1)} %reshape.119, bf16[]{:T(256)} %constant.8.clone.1), kind=kCustom, calls=%fused_computation.25 | custom fusion | bytes 524800 | tf_op jit(solution)/shard_map/scatter | solution.py:40
  15.1 1.7 %all-to-all-done.2 = bf16[32,2,512]{2,1,0:T(2,128)(2,1)S(1)} async-done(((bf16[32,2,512]{2,1,0:T(2,128)(2,1)}), bf16[32,2,512]{2,1,0:T(2,128)(2,1)S(1)}, u32[]{:S(2)}, u32[]{:S(2)}) %all-to-all-start.2) | async-done | bytes 65568 | tf_op jit(solution)/shard_map/all_to_all | solution.py:60
  16.8 1.1 broadcast_in_dim.23
  17.9 4.3 %all-to-all-start = ((bf16[32,8,2048]{2,1,0:T(8,128)(2,1)}), bf16[32,8,2048]{2,1,0:T(8,128)(2,1)}, u32[]{:S(2)}, u32[]{:S(2)}) async-start(bf16[32,8,2048]{2,1,0:T(8,128)(2,1)} %bitcast.67), calls=%async_computation | async-start | bytes 2097152 | tf_op jit(solution)/shard_map/all_to_all | solution.py:46
  22.1 0.0 copy-start.2
  22.2 2.8 %copy.25 = bf16[64,8192]{0,1:T(8,128)(2,1)} copy(bf16[64,8192]{1,0:T(8,128)(2,1)} %param.16) | data formatting | bytes 2097152 | tf_op args[7]
  24.9 2.8 %copy.27 = bf16[64,8192]{0,1:T(8,128)(2,1)} copy(bf16[64,8192]{1,0:T(8,128)(2,1)} %param.17) | data formatting | bytes 2097152 | tf_op args[8]
  27.7 0.0 copy-done.2
  27.7 3.9 %gather_fusion.1 = bf16[512,64,16]{1,2,0:T(8,128)(2,1)} fusion(bf16[64,512,16]{0,2,1:T(8,128)(2,1)} %bitcast.65, s32[1024]{0:T(1024)S(1)} %pad_clamp_fusion), kind=kCustom, calls=%fused_computation.1 | custom fusion | bytes 2099200 | tf_op jit(solution)/shard_map/gather | solution.py:63
  31.6 4.0 %gather_fusion.2 = bf16[512,64,16]{1,2,0:T(8,128)(2,1)} fusion(bf16[64,512,16]{0,2,1:T(8,128)(2,1)} %bitcast.64, s32[1024]{0:T(1024)S(1)} %pad_clamp_fusion), kind=kCustom, calls=%fused_computation.2 | custom fusion | bytes 2099200 | tf_op jit(solution)/shard_map/gather | solution.py:70
  35.6 0.1 reshape.133
  35.8 2.8 %fusion.11 = f32[512,1,16]{2,1,0:T(1,128)S(1)} fusion(bf16[512,64,16]{1,2,0:T(8,128)(2,1)} %gather_fusion.1, bf16[512,64,1]{1,0,2:T(8,128)(2,1)S(1)} %bitcast.74), kind=kOutput, calls=%fused_computation.14 | convolution fusion | flops 1048576 | bytes 1146880 | tf_op jit(solution)/shard_map/tf,ftr->tr/dot_general | solution.py:66
  38.5 43.0 %psum.7 = bf16[512,16]{1,0:T(8,128)(2,1)S(1)} all-reduce(f32[512,16]{1,0:T(8,128)S(1)} %bitcast.71), channel_id=1, replica_groups=mesh['grp'=1,'exp'=32] {'exp'}, use_global_device_ids=true, to_apply=%region_5.6 | all-reduce | flops 8192 | bytes 49152 | tf_op jit(solution)/shard_map/psum | solution.py:69
  81.6 2.3 %fusion.9 = f32[512,1,64]{2,1,0:T(1,128)S(1)} fusion(bf16[512,64,16]{1,2,0:T(8,128)(2,1)} %gather_fusion.2, bf16[512,16,1]{1,0,2:T(8,128)(2,1)S(1)} %bitcast.73), kind=kOutput, calls=%fused_computation.12 | convolution fusion | flops 1048576 | bytes 1196032 | tf_op jit(solution)/shard_map/tr,ftr->tf/dot_general | solution.py:73
  83.9 0.8 reshape.134
  84.6 0.0 all-to-all-done
  84.6 3.9 %all-to-all-start.3 = ((bf16[32,2,512]{2,1,0:T(2,128)(2,1)}), bf16[32,2,512]{2,1,0:T(2,128)(2,1)S(1)}, u32[]{:S(2)}, u32[]{:S(2)}) async-start(bf16[32,2,512]{2,1,0:T(2,128)(2,1)} %reshape.134), calls=%async_computation.3 | async-start | bytes 131072 | tf_op jit(solution)/shard_map/all_to_all | solution.py:76
  88.5 0.0 copy-start.3
  88.5 3.2 %fusion.4 = f32[256,704]{0,1:T(8,128)S(1)} fusion(bf16[1,2048,704]{1,2,0:T(8,128)(2,1)} %param.13, bf16[32,8,2048]{2,1,0:T(8,128)(2,1)} %all-to-all-done), kind=kOutput, calls=%fused_computation.8 | convolution fusion | flops 738197504 | bytes 4653056 | tf_op jit(solution)/shard_map/dot_general | solution.py:11
  91.8 0.0 copy-done.3
  91.8 2.9 %fusion.16 = bf16[256,704]{0,1:T(8,128)(2,1)} fusion(bf16[1,2048,704]{1,2,0:T(8,128)(2,1)S(1)} %copy-done.3, bf16[32,8,2048]{2,1,0:T(8,128)(2,1)} %all-to-all-done, f32[256,704]{0,1:T(8,128)S(1)} %fusion.4), kind=kOutput, calls=%fused_computation.17 | convolution fusion | flops 739278848 | bytes 5013504 | tf_op jit(solution)/shard_map/dot_general | solution.py:12
  94.7 1.2 copy.23
  95.8 0.0 copy-done
  95.8 0.0 copy-start.1
  95.9 2.0 %fusion.6 = bf16[32,8,2048]{2,1,0:T(8,128)(2,1)} fusion(bf16[1,704,2048]{2,1,0:T(8,128)(2,1)S(1)} %copy-done, bf16[256,704]{1,0:T(8,128)(2,1)S(1)} %copy.23), kind=kOutput, calls=%fused_computation.10 | convolution fusion | flops 738721792 | bytes 4292608 | tf_op jit(solution)/shard_map/dot_general | solution.py:14
  97.9 0.0 all-to-all-done.3
  97.9 6.0 %all-to-all-start.1 = ((bf16[32,8,2048]{2,1,0:T(8,128)(2,1)}), bf16[32,8,2048]{2,1,0:T(8,128)(2,1)}, u32[]{:S(2)}, u32[]{:S(2)}) async-start(bf16[32,8,2048]{2,1,0:T(8,128)(2,1)} %fusion.6), calls=%async_computation.1 | async-start | bytes 2097152 | tf_op jit(solution)/shard_map/all_to_all | solution.py:53
  103.9 0.0 copy-done.1
  103.9 0.1 copy.24
  104.0 0.1 reshape.135
  104.1 0.1 copy.28
  104.2 0.1 reshape.90
  104.3 25.7 %all-to-all-done.1 = bf16[32,8,2048]{2,1,0:T(8,128)(2,1)} async-done(((bf16[32,8,2048]{2,1,0:T(8,128)(2,1)}), bf16[32,8,2048]{2,1,0:T(8,128)(2,1)}, u32[]{:S(2)}, u32[]{:S(2)}) %all-to-all-start.1) | async-done | bytes 1048608 | tf_op jit(solution)/shard_map/all_to_all | solution.py:53
  130.0 2.5 %convert_reduce_fusion = f32[16,8,2048]{2,1,0:T(8,128)} fusion(bf16[32,8,2048]{2,1,0:T(8,128)(2,1)} %all-to-all-done.1), kind=kLoop, calls=%fused_computation.11 | loop fusion | flops 786432 | bytes 2097152 | tf_op jit(solution)/shard_map/reduce_sum | solution.py:56
  132.6 3.3 %gather_fusion = f32[96,2048]{1,0:T(8,128)} fusion(f32[128,2048]{1,0:T(8,128)} %bitcast.66, s32[1024]{0:T(1024)S(1)} %pad_clamp_fusion.1), kind=kCustom, calls=%fused_computation | custom fusion | bytes 1573248 | tf_op jit(solution)/shard_map/gather | solution.py:58
  135.9 2.2 %gather.12 = f32[16,6,2048]{2,1,0:T(8,128)} reshape(f32[96,2048]{1,0:T(8,128)} %gather_fusion) | data formatting | bytes 1572864 | tf_op jit(solution)/shard_map/gather | solution.py:58
  138.1 1.6 %multiply_reduce_fusion = f32[16,2048]{1,0:T(8,128)S(1)} fusion(f32[16,6,2048]{2,1,0:T(8,128)} %gather.12, f32[16,6]{1,0:T(8,128)S(1)} %copy.24), kind=kLoop, calls=%fused_computation.20 | loop fusion | flops 360448 | bytes 917888 | tf_op jit(solution)/shard_map/reduce_sum | solution.py:59
  139.7 0.6 add_convert_fusion
  (6 shorter events, 0.1 us)
Async XLA Ops:
  0.0 95.8 %copy-start = (bf16[1,704,2048]{2,1,0:T(8,128)(2,1)S(1)}, bf16[1,704,2048]{2,1,0:T(8,128)(2,1)}, u32[]{:S(2)}) copy-start(bf16[1,704,2048]{2,1,0:T(8,128)(2,1)} %param.15) | copy-start | bytes 8650756
  2.0 14.7 %all-to-all-start.2 = ((bf16[32,2,512]{2,1,0:T(2,128)(2,1)}), bf16[32,2,512]{2,1,0:T(2,128)(2,1)S(1)}, u32[]{:S(2)}, u32[]{:S(2)}) async-start(bf16[32,2,512]{2,1,0:T(2,128)(2,1)} %reshape.132), calls=%async_computation.2 | async-start | bytes 131072 | tf_op jit(solution)/shard_map/all_to_all | solution.py:60
  17.9 66.8 %all-to-all-start = ((bf16[32,8,2048]{2,1,0:T(8,128)(2,1)}), bf16[32,8,2048]{2,1,0:T(8,128)(2,1)}, u32[]{:S(2)}, u32[]{:S(2)}) async-start(bf16[32,8,2048]{2,1,0:T(8,128)(2,1)} %bitcast.67), calls=%async_computation | async-start | bytes 2097152 | tf_op jit(solution)/shard_map/all_to_all | solution.py:46
  22.1 5.6 %copy-start.2 = (s32[512]{0:T(512)S(1)}, s32[512]{0:T(512)}, u32[]{:S(2)}) copy-start(s32[512]{0:T(512)} %param.12) | copy-start | bytes 6148
  84.6 13.3 %all-to-all-start.3 = ((bf16[32,2,512]{2,1,0:T(2,128)(2,1)}), bf16[32,2,512]{2,1,0:T(2,128)(2,1)S(1)}, u32[]{:S(2)}, u32[]{:S(2)}) async-start(bf16[32,2,512]{2,1,0:T(2,128)(2,1)} %reshape.134), calls=%async_computation.3 | async-start | bytes 131072 | tf_op jit(solution)/shard_map/all_to_all | solution.py:76
  88.5 3.3 %copy-start.3 = (bf16[1,2048,704]{1,2,0:T(8,128)(2,1)S(1)}, bf16[1,2048,704]{1,2,0:T(8,128)(2,1)}, u32[]{:S(2)}) copy-start(bf16[1,2048,704]{1,2,0:T(8,128)(2,1)} %param.14) | copy-start | bytes 8650756
  95.8 8.0 %copy-start.1 = (f32[16,6]{0,1:T(8,128)S(1)}, f32[16,6]{0,1:T(8,128)}, u32[]{:S(2)}) copy-start(f32[16,6]{0,1:T(8,128)} %param.11) | copy-start | bytes 1156
  97.9 32.1 %all-to-all-start.1 = ((bf16[32,8,2048]{2,1,0:T(8,128)(2,1)}), bf16[32,8,2048]{2,1,0:T(8,128)(2,1)}, u32[]{:S(2)}, u32[]{:S(2)}) async-start(bf16[32,8,2048]{2,1,0:T(8,128)(2,1)} %fusion.6), calls=%async_computation.1 | async-start | bytes 2097152 | tf_op jit(solution)/shard_map/all_to_all | solution.py:53
where the time goes:
time: 141 us; the launch traced here: 140 us
  blocking collectives  43 us (30%)
  local copies, waits for them, and re-layouts  29.2 us (21%)
  waiting for transfers between devices  27.4 us (19%)
  starting transfers between devices  21.4 us (15%)
  matrix products  13.2 us (9%)
  other arithmetic  5.94 us (4%)
    psum x1, blocking collectives, per_device(): gathered_ranks = lax.psum(rank_terms, 'exp').astype(jnp.bfloat16)  43 us
    all_to_all x1, waiting for transfers between devices, per_device(): lax.all_to_all(partial_value.astype(jnp.bfloat16), 'exp', split_axis=0, c...  25.7 us
    unnamed x16, local copies, waits for them, and re-layouts  8.22 us
    all_to_all x1, starting transfers between devices, per_device(): lax.all_to_all(tokens, 'exp', split_axis=1, concat_axis=0, tiled=True)  7.33 us
    all_to_all x1, starting transfers between devices, per_device(): lax.all_to_all(partial_value.astype(jnp.bfloat16), 'exp', split_axis=0, c...  5.96 us
    gather x2, local copies, waits for them, and re-layouts, per_device(): picked = gather_results[slots] * gate_col  5.55 us
    all_to_all x1, starting transfers between devices, per_device(): lax.all_to_all(doubled, 'exp', split_axis=0, concat_axis=0, tiled=True)  4.27 us
    gather x1, local copies, waits for them, and re-layouts, per_device(): adapter_up_matrix.reshape(feature_rows, adapter_table, ADAPTER_RANK)  3.97 us
  transfers between devices with their start and end apart: 4, of which 2 were waited for; matrix products, arithmetic and copies ran while one was open for 25% of the time, Pallas kernels for 0%

commit v1 on v0

--- a/solution.py
+++ b/solution.py
@@ -66,7 +66,7 @@
     rank_terms = jnp.einsum(
         "tf,ftr->tr", columns, down_selected, preferred_element_type=jnp.float32
     )
-    gathered_ranks = lax.psum(rank_terms, "exp").astype(jnp.bfloat16)
+    gathered_ranks = jnp.sum(lax.all_gather(rank_terms, "exp"), axis=0).astype(jnp.bfloat16)
     up_selected = adapter_up_matrix.reshape(feature_rows, adapter_table, ADAPTER_RANK)[
         :, token_adapter_index, :
     ]

time: 141 us -> 159 us (1.13)
  waiting for transfers between devices: 27.4 us -> 73.6 us
  blocking collectives: 43 us -> 0 us
  between operations: 0.22 us -> 13.6 us
  local copies, waits for them, and re-layouts: 29.2 us -> 32.7 us
  starting transfers between devices: 21.4 us -> 18.6 us
    psum x1 -> x0, blocking collectives: 43 us -> none  [per_device(): gathered_ranks = lax.psum(rank_terms, 'exp').astype(jnp.bfloat16)]
    all_gather x0 -> x1, waiting for transfers between devices: none -> 31.6 us  [per_device(): lax.all_gather(rank_terms, 'exp')]
    all_to_all x1, waiting for transfers between devices: 0.01 us -> 9.21 us  [per_device(): lax.all_to_all(doubled, 'exp', split_axis=0, concat_axis=0, tiled=True)]
    all_to_all x1, waiting for transfers between devices: 0.01 us -> 5.36 us  [per_device(): lax.all_to_all(correction_cols.astype(jnp.bfloat16), 'exp', split_axis=0,...]
    all_to_all x1, starting transfers between devices: 5.96 us -> 3.38 us  [per_device(): lax.all_to_all(partial_value.astype(jnp.bfloat16), 'exp', split_axis=0, c...]
    unnamed x16 -> x17, local copies, waits for them, and re-layouts: 8.22 us -> 10 us
  transfers between devices with their start and end apart: 4 -> 5, of which waited for: 2 -> 5; matrix products, arithmetic and copies ran while one was open for 25% -> 21% of each run, Pallas kernels for 0% -> 0%
where the time goes in v1:
time: 159 us; the launch traced here: 158 us
  waiting for transfers between devices  73.6 us (46%)
  local copies, waits for them, and re-layouts  32.7 us (21%)
  starting transfers between devices  18.6 us (12%)
  between operations  13.6 us (9%)
  matrix products  13.3 us (8%)
  other arithmetic  6.04 us (4%)
    all_gather x1, waiting for transfers between devices, per_device(): lax.all_gather(rank_terms, 'exp')  31.6 us
    all_to_all x1, waiting for transfers between devices, per_device(): lax.all_to_all(partial_value.astype(jnp.bfloat16), 'exp', split_axis=0, c...  25.7 us
    unnamed x17, local copies, waits for them, and re-layouts  10 us
    all_to_all x1, waiting for transfers between devices, per_device(): lax.all_to_all(doubled, 'exp', split_axis=0, concat_axis=0, tiled=True)  9.21 us
    all_to_all x1, starting transfers between devices, per_device(): lax.all_to_all(tokens, 'exp', split_axis=1, concat_axis=0, tiled=True)  7.33 us
    gather x2, local copies, waits for them, and re-layouts, per_device(): picked = gather_results[slots] * gate_col  5.55 us
    all_to_all x1, waiting for transfers between devices, per_device(): lax.all_to_all(correction_cols.astype(jnp.bfloat16), 'exp', split_axis=0,...  5.36 us
    all_to_all x1, starting transfers between devices, per_device(): lax.all_to_all(doubled, 'exp', split_axis=0, concat_axis=0, tiled=True)  4.27 us
  transfers between devices with their start and end apart: 5, of which 5 were waited for; matrix products, arithmetic and copies ran while one was open for 21% of the time, Pallas kernels for 0%

profile of v1, /device:TPU:0, one launch (start us, length us, event | category | flops | bytes accessed | tf_op | source)
XLA Modules:
  0.0 157.8 jit_solution(2687017034624206270)
XLA Ops:
  6.5 0.0 copy-start
  6.5 1.2 all_to_all.32
  7.7 0.1 copy.47
  7.8 0.8 reshape.133
  8.5 7.3 %all-to-all-start.2 = ((bf16[32,2,512]{2,1,0:T(2,128)(2,1)}), bf16[32,2,512]{2,1,0:T(2,128)(2,1)S(1)}, u32[]{:S(2)}, u32[]{:S(2)}) async-start(bf16[32,2,512]{2,1,0:T(2,128)(2,1)} %reshape.133), calls=%async_computation.2 | async-start | bytes 131072 | tf_op jit(solution)/shard_map/all_to_all | solution.py:60
  15.9 0.7 broadcast_multiply_fusion
  16.6 0.8 copy.30
  17.3 0.1 copy.29
  17.4 0.1 mul.37
  17.5 0.1 eq.15
  17.6 0.1 fusion.25
  17.7 0.1 reduce_window_sum.11
  17.8 0.2 select_reduce_fusion
  18.0 0.9 broadcast_in_dim.21
  18.9 0.9 reshape.119
  19.8 1.8 %scatter_custom_fusion = bf16[128,2048]{1,0:T(8,128)(2,1)S(1)} fusion(s32[96]{0:T(128)S(1)} %fusion.26, bf16[96,2048]{1,0:T(8,128)(2,1)} %reshape.119, bf16[]{:T(256)} %constant.8.clone.1), kind=kCustom, calls=%fused_computation.25 | custom fusion | bytes 524800 | tf_op jit(solution)/shard_map/scatter | solution.py:40
  21.6 1.7 %all-to-all-done.2 = bf16[32,2,512]{2,1,0:T(2,128)(2,1)S(1)} async-done(((bf16[32,2,512]{2,1,0:T(2,128)(2,1)}), bf16[32,2,512]{2,1,0:T(2,128)(2,1)S(1)}, u32[]{:S(2)}, u32[]{:S(2)}) %all-to-all-start.2) | async-done | bytes 65568 | tf_op jit(solution)/shard_map/all_to_all | solution.py:60
  23.3 1.1 broadcast_in_dim.23
  24.4 0.0 copy-start.2
  24.4 4.3 %all-to-all-start = ((bf16[32,8,2048]{2,1,0:T(8,128)(2,1)}), bf16[32,8,2048]{2,1,0:T(8,128)(2,1)}, u32[]{:S(2)}, u32[]{:S(2)}) async-start(bf16[32,8,2048]{2,1,0:T(8,128)(2,1)} %bitcast.72), calls=%async_computation | async-start | bytes 2097152 | tf_op jit(solution)/shard_map/all_to_all | solution.py:46
  28.7 0.0 all-gather.3.cloned.1.call-start
  28.8 2.8 %copy.33 = bf16[64,8192]{0,1:T(8,128)(2,1)} copy(bf16[64,8192]{1,0:T(8,128)(2,1)} %param.16) | data formatting | bytes 2097152 | tf_op args[7]
  31.6 0.0 copy-done.2
  31.6 3.9 %gather_fusion.1 = bf16[512,64,16]{1,2,0:T(8,128)(2,1)} fusion(bf16[64,512,16]{0,2,1:T(8,128)(2,1)} %bitcast.69, s32[1024]{0:T(1024)S(1)} %pad_clamp_fusion), kind=kCustom, calls=%fused_computation.1 | custom fusion | bytes 2099200 | tf_op jit(solution)/shard_map/gather | solution.py:63
  35.5 0.1 reshape.134
  35.6 2.8 %fusion.11 = f32[512,1,16]{2,1,0:T(1,128)S(1)} fusion(bf16[512,64,16]{1,2,0:T(8,128)(2,1)} %gather_fusion.1, bf16[512,64,1]{1,0,2:T(8,128)(2,1)S(1)} %bitcast.79), kind=kOutput, calls=%fused_computation.14 | convolution fusion | flops 1048576 | bytes 1146880 | tf_op jit(solution)/shard_map/tf,ftr->tr/dot_general | solution.py:66
  38.4 0.7 copy.39
  39.2 0.0 all-gather.3.cloned.1.call-update
  39.2 2.7 %copy.36 = bf16[64,8192]{0,1:T(8,128)(2,1)} copy(bf16[64,8192]{1,0:T(8,128)(2,1)} %param.17) | data formatting | bytes 2097152 | tf_op args[8]
  41.9 4.0 %gather_fusion.2 = bf16[512,64,16]{1,2,0:T(8,128)(2,1)} fusion(bf16[64,512,16]{0,2,1:T(8,128)(2,1)} %bitcast.70, s32[1024]{0:T(1024)S(1)} %pad_clamp_fusion), kind=kCustom, calls=%fused_computation.2 | custom fusion | bytes 2099200 | tf_op jit(solution)/shard_map/gather | solution.py:70
  45.9 9.2 %all-to-all-done = bf16[32,8,2048]{2,1,0:T(8,128)(2,1)} async-done(((bf16[32,8,2048]{2,1,0:T(8,128)(2,1)}), bf16[32,8,2048]{2,1,0:T(8,128)(2,1)}, u32[]{:S(2)}, u32[]{:S(2)}) %all-to-all-start) | async-done | bytes 1048608 | tf_op jit(solution)/shard_map/all_to_all | solution.py:46
  55.1 0.0 copy-start.3
  55.1 3.2 %fusion.4 = f32[256,704]{0,1:T(8,128)S(1)} fusion(bf16[1,2048,704]{1,2,0:T(8,128)(2,1)} %param.13, bf16[32,8,2048]{2,1,0:T(8,128)(2,1)} %all-to-all-done), kind=kOutput, calls=%fused_computation.8 | convolution fusion | flops 738197504 | bytes 4653056 | tf_op jit(solution)/shard_map/dot_general | solution.py:11
  58.4 0.0 copy-done.3
  58.4 2.9 %fusion.16 = bf16[256,704]{0,1:T(8,128)(2,1)} fusion(bf16[1,2048,704]{1,2,0:T(8,128)(2,1)S(1)} %copy-done.3, bf16[32,8,2048]{2,1,0:T(8,128)(2,1)} %all-to-all-done, f32[256,704]{0,1:T(8,128)S(1)} %fusion.4), kind=kOutput, calls=%fused_computation.17 | convolution fusion | flops 739278848 | bytes 5013504 | tf_op jit(solution)/shard_map/dot_general | solution.py:12
  61.3 1.2 copy.31
  62.4 31.6 %all-gather.3.cloned.1.call-done = f32[16384,16]{0,1:T(8,128)} async-done(((f32[512,16]{0,1:T(8,128)}), f32[16384,16]{0,1:T(8,128)}) %all-gather.3.cloned.1.call-update) | async-done | bytes 1048592 | tf_op jit(solution)/shard_map/all_gather | solution.py:69
  94.0 1.8 %copy.43 = f32[2,8,32,512]{3,2,1,0:T(8,128)S(1)} copy(f32[2,8,32,512]{3,1,2,0:T(8,128)} %bitcast.74) | data formatting | bytes 2097152
  95.9 0.1 bitcast_reduce_fusion
  96.0 0.9 copy.40
  96.9 2.4 %fusion.9 = f32[512,1,64]{2,1,0:T(1,128)S(1)} fusion(bf16[512,16,1]{1,2,0:T(2,128)(2,1)} %copy.40, bf16[512,64,16]{1,2,0:T(8,128)(2,1)} %gather_fusion.2), kind=kOutput, calls=%fused_computation.12 | convolution fusion | flops 1048576 | bytes 1196032 | tf_op jit(solution)/shard_map/tr,ftr->tf/dot_general | solution.py:73
  99.3 0.8 reshape.135
  100.0 3.6 %all-to-all-start.3 = ((bf16[32,2,512]{2,1,0:T(2,128)(2,1)}), bf16[32,2,512]{2,1,0:T(2,128)(2,1)S(1)}, u32[]{:S(2)}, u32[]{:S(2)}) async-start(bf16[32,2,512]{2,1,0:T(2,128)(2,1)} %reshape.135), calls=%async_computation.3 | async-start | bytes 131072 | tf_op jit(solution)/shard_map/all_to_all | solution.py:76
  103.7 0.0 copy-done
  103.7 0.0 copy-start.1
  103.7 2.0 %fusion.6 = bf16[32,8,2048]{2,1,0:T(8,128)(2,1)} fusion(bf16[1,704,2048]{2,1,0:T(8,128)(2,1)S(1)} %copy-done, bf16[256,704]{1,0:T(8,128)(2,1)S(1)} %copy.31), kind=kOutput, calls=%fused_computation.10 | convolution fusion | flops 738721792 | bytes 4292608 | tf_op jit(solution)/shard_map/dot_general | solution.py:14
  105.7 5.4 %all-to-all-done.3 = bf16[32,2,512]{2,1,0:T(2,128)(2,1)S(1)} async-done(((bf16[32,2,512]{2,1,0:T(2,128)(2,1)}), bf16[32,2,512]{2,1,0:T(2,128)(2,1)S(1)}, u32[]{:S(2)}, u32[]{:S(2)}) %all-to-all-start.3) | async-done | bytes 65568 | tf_op jit(solution)/shard_map/all_to_all | solution.py:76
  111.1 3.4 %all-to-all-start.1 = ((bf16[32,8,2048]{2,1,0:T(8,128)(2,1)}), bf16[32,8,2048]{2,1,0:T(8,128)(2,1)}, u32[]{:S(2)}, u32[]{:S(2)}) async-start(bf16[32,8,2048]{2,1,0:T(8,128)(2,1)} %fusion.6), calls=%async_computation.1 | async-start | bytes 2097152 | tf_op jit(solution)/shard_map/all_to_all | solution.py:53
  114.5 0.0 copy-done.1
  114.5 0.1 copy.32
  114.6 0.1 reshape.136
  114.7 0.1 copy.37
  114.8 0.1 reshape.90
  114.9 25.7 %all-to-all-done.1 = bf16[32,8,2048]{2,1,0:T(8,128)(2,1)} async-done(((bf16[32,8,2048]{2,1,0:T(8,128)(2,1)}), bf16[32,8,2048]{2,1,0:T(8,128)(2,1)}, u32[]{:S(2)}, u32[]{:S(2)}) %all-to-all-start.1) | async-done | bytes 1048608 | tf_op jit(solution)/shard_map/all_to_all | solution.py:53
  140.6 2.5 %convert_reduce_fusion = f32[16,8,2048]{2,1,0:T(8,128)} fusion(bf16[32,8,2048]{2,1,0:T(8,128)(2,1)} %all-to-all-done.1), kind=kLoop, calls=%fused_computation.11 | loop fusion | flops 786432 | bytes 2097152 | tf_op jit(solution)/shard_map/reduce_sum | solution.py:56
  143.2 3.3 %gather_fusion = f32[96,2048]{1,0:T(8,128)} fusion(f32[128,2048]{1,0:T(8,128)} %bitcast.71, s32[1024]{0:T(1024)S(1)} %pad_clamp_fusion.1), kind=kCustom, calls=%fused_computation | custom fusion | bytes 1573248 | tf_op jit(solution)/shard_map/gather | solution.py:58
  146.5 2.2 %gather.12 = f32[16,6,2048]{2,1,0:T(8,128)} reshape(f32[96,2048]{1,0:T(8,128)} %gather_fusion) | data formatting | bytes 1572864 | tf_op jit(solution)/shard_map/gather | solution.py:58
  148.7 1.6 %multiply_reduce_fusion = f32[16,2048]{1,0:T(8,128)S(1)} fusion(f32[16,6,2048]{2,1,0:T(8,128)} %gather.12, f32[16,6]{1,0:T(8,128)S(1)} %copy.32), kind=kLoop, calls=%fused_computation.21 | loop fusion | flops 360448 | bytes 917888 | tf_op jit(solution)/shard_map/reduce_sum | solution.py:59
  150.3 0.6 add_convert_fusion
  (6 shorter events, 0.1 us)
Async XLA Ops:
  6.5 97.1 %copy-start = (bf16[1,704,2048]{2,1,0:T(8,128)(2,1)S(1)}, bf16[1,704,2048]{2,1,0:T(8,128)(2,1)}, u32[]{:S(2)}) copy-start(bf16[1,704,2048]{2,1,0:T(8,128)(2,1)} %param.15) | copy-start | bytes 8650756
  8.5 14.7 %all-to-all-start.2 = ((bf16[32,2,512]{2,1,0:T(2,128)(2,1)}), bf16[32,2,512]{2,1,0:T(2,128)(2,1)S(1)}, u32[]{:S(2)}, u32[]{:S(2)}) async-start(bf16[32,2,512]{2,1,0:T(2,128)(2,1)} %reshape.133), calls=%async_computation.2 | async-start | bytes 131072 | tf_op jit(solution)/shard_map/all_to_all | solution.py:60
  24.4 7.1 %copy-start.2 = (s32[512]{0:T(512)S(1)}, s32[512]{0:T(512)}, u32[]{:S(2)}) copy-start(s32[512]{0:T(512)} %param.12) | copy-start | bytes 6148
  24.4 30.7 %all-to-all-start = ((bf16[32,8,2048]{2,1,0:T(8,128)(2,1)}), bf16[32,8,2048]{2,1,0:T(8,128)(2,1)}, u32[]{:S(2)}, u32[]{:S(2)}) async-start(bf16[32,8,2048]{2,1,0:T(8,128)(2,1)} %bitcast.72), calls=%async_computation | async-start | bytes 2097152 | tf_op jit(solution)/shard_map/all_to_all | solution.py:46
  28.7 65.3 %all-gather.3.cloned.1.call-start = ((), (), s32[]{:S(2)}) async-start(), calls=%async_computation.4 | async-start | bytes 1081344 | tf_op jit(solution)/shard_map/all_gather | solution.py:69
  55.1 3.2 %copy-start.3 = (bf16[1,2048,704]{1,2,0:T(8,128)(2,1)S(1)}, bf16[1,2048,704]{1,2,0:T(8,128)(2,1)}, u32[]{:S(2)}) copy-start(bf16[1,2048,704]{1,2,0:T(8,128)(2,1)} %param.14) | copy-start | bytes 8650756
  100.0 11.0 %all-to-all-start.3 = ((bf16[32,2,512]{2,1,0:T(2,128)(2,1)}), bf16[32,2,512]{2,1,0:T(2,128)(2,1)S(1)}, u32[]{:S(2)}, u32[]{:S(2)}) async-start(bf16[32,2,512]{2,1,0:T(2,128)(2,1)} %reshape.135), calls=%async_computation.3 | async-start | bytes 131072 | tf_op jit(solution)/shard_map/all_to_all | solution.py:76
  103.7 10.8 %copy-start.1 = (f32[16,6]{0,1:T(8,128)S(1)}, f32[16,6]{0,1:T(8,128)}, u32[]{:S(2)}) copy-start(f32[16,6]{0,1:T(8,128)} %param.11) | copy-start | bytes 1156
  111.1 29.6 %all-to-all-start.1 = ((bf16[32,8,2048]{2,1,0:T(8,128)(2,1)}), bf16[32,8,2048]{2,1,0:T(8,128)(2,1)}, u32[]{:S(2)}, u32[]{:S(2)}) async-start(bf16[32,8,2048]{2,1,0:T(8,128)(2,1)} %fusion.6), calls=%async_computation.1 | async-start | bytes 2097152 | tf_op jit(solution)/shard_map/all_to_all | solution.py:53
Sparse Core Ops, SparseCore 0:
  39.3 54.6 all-gather.2
